TPU v7x, 512 devices: a whole 4x4x16 slice. The times are simulated.
512 devices in a mesh: ga: 32 (over y, x, core), ka: 16 (over z).
Axes of the slice: x: 4, y: 4, z: 16, core: 2. Of those that a mesh axis runs over, the one named last changes fastest.
Arguments:
- fine_waves: bfloat16 [256, 16, 40960], P('ka', None, 'ga'), may hold values from -6 to 6
- coarse_waves: bfloat16 [128, 16, 40960], P('ka', None, 'ga'), may hold values from -6 to 6
- coarse_kernel: bfloat16 [192, 64, 8192], P('ga', None, 'ka'), may hold values from -6 to 6
- row_valence: float32 [32, 8, 8, 8], P('ga'), may hold values from -6 to 6
- row_conduction: float32 [32, 8, 8, 8], P('ga'), may hold values from -6 to 6
- row_neighbours: int32 [32, 8], P('ga'), may hold values from 0 to 11, as said below
- row_weight_index: int32 [32, 8], P('ga'), may hold values from 0 to 7
- col_neighbours: int32 [256, 8], P('ka'), may hold values from 0 to 31, as said below
- col_weight_index: int32 [256, 8], P('ka'), may hold values from 0 to 7
- tile_list: int32 [16, 32], replicated, may hold values from 0 to 127, as said below
- weight_table: float32 [8], replicated, may hold values from 0.2 to 0.5
Outputs:
- fine_kernel: bfloat16 [32, 256, 4096], P('ga', 'ka')
Inputs may be any that keep to these rules, and one draw needn't show every extreme that they name: `row_neighbours`: each row names 8 distinct positions; a position p below 6 is coarse row p of the fine row's own group r, a larger one is coarse row p - 6 of the next group (the last group's next is group 0); each row names three or more of each kind. `col_neighbours`: each fine column names 8 distinct positions of its owner's list, and every position of the list is named by some column of that owner. `tile_list`: row o lists 32 distinct coarse columns in rising order of their holder (column p is held by owner p // 8); no row takes more than 4 columns from one holder, and every row takes exactly 4 from some holder.
All inputs are finite; a program needn't handle non-finite values.
Results may differ from a plain program's by a relative error of at most 0.0064.
Values may be sent and summed in bfloat16 or wider, within the bound.
A program may use at most 64 MiB of HBM per device.

v0:
```python
import math

import jax
import jax.numpy as jnp
from jax import lax
from jax.sharding import PartitionSpec as P

VALENCE = 8
PLANE_WAVES = 40960
CORNERS = 8
BAND_PAIRS = 64
SLOT_COUNT = 4


def sent_to_all(array, axis):
    peers = lax.axis_size(axis)
    return lax.all_to_all(
        jnp.broadcast_to(array[None], (peers, *array.shape)), axis, 0, 0, tiled=True
    )


def over_copies(array, axis):
    everything = sent_to_all(array, axis)
    return jnp.sum(everything, axis=0)


def in_one(arrays, axis):
    flat, at, gathered = (jnp.concatenate([a.reshape(-1) for a in arrays]), 0, [])
    subtotal = over_copies(flat, axis)
    for a in arrays:
        gathered.append(subtotal[at : at + a.size].reshape(a.shape))
        at += a.size
    return tuple(gathered)


def passed_along(array, axis, by):
    peers = lax.axis_size(axis)
    return lax.ppermute(array, axis, [(i, (i + by) % peers) for i in range(peers)])


def table_lookup(indices, weight_table):
    levels = jnp.arange(weight_table.shape[0], dtype=jnp.int32)
    return jnp.sum(jnp.where(indices[..., None] == levels, weight_table, 0.0), axis=-1)


def pair_tiles(weights, valence_sel, conduction_sel):
    lead = valence_sel.shape[:2]
    outer_product = valence_sel[:, :, :, None, :, None] * conduction_sel[:, :, None, :, None, :]
    outer_product = outer_product.reshape(lead + (BAND_PAIRS, BAND_PAIRS))
    scaled = weights[:, :, None, None] * outer_product / math.sqrt(BAND_PAIRS)
    return scaled.astype(jnp.bfloat16)


def slot_tables(tile_list, owner_index, held_cols, slot_count):
    owner_count, list_length = tile_list.shape
    holders = tile_list // held_cols
    positions = jnp.arange(list_length, dtype=jnp.int32)
    earlier = positions[None, :] < positions[:, None]
    shared_holder = holders[:, :, None] == holders[:, None, :]
    rank_in_list = jnp.sum(jnp.logical_and(shared_holder, earlier[None]), axis=2)
    mine_holders = lax.dynamic_index_in_dim(holders, owner_index, 0, keepdims=False)
    mine_ranks = lax.dynamic_index_in_dim(rank_in_list, owner_index, 0, keepdims=False)
    arrival = mine_holders * slot_count + mine_ranks
    slot_ids = jnp.arange(slot_count, dtype=jnp.int32)
    matches = jnp.logical_and(
        (holders == owner_index)[:, :, None], rank_in_list[:, :, None] == slot_ids
    )
    local_ids = (tile_list - owner_index * held_cols)[:, :, None]
    departure = jnp.sum(jnp.where(matches, local_ids, 0), axis=1).reshape(owner_count * slot_count)
    return (departure, arrival)


def band_correlations(fine_part, list_part, col_neighbours):
    fine_count, bands, wave_count = fine_part.shape
    list_length = list_part.shape[0]
    corner_count = col_neighbours.shape[1]
    dense = jnp.dot(
        fine_part.reshape(fine_count * bands, wave_count),
        list_part.reshape(list_length * bands, wave_count).T,
        preferred_element_type=jnp.float32,
    )
    dense = dense.reshape(fine_count, bands, list_length, bands)
    picks = jnp.broadcast_to(
        col_neighbours[:, None, :, None], (fine_count, bands, corner_count, bands)
    )
    chosen = jnp.take_along_axis(dense, picks, axis=2)
    return jnp.transpose(chosen, (0, 2, 1, 3))


def rotate_rows(stacked, row_mats, row_neighbours):
    chosen = jnp.take(stacked, row_neighbours[0], axis=0).reshape(row_mats.shape[2], -1)
    product = jnp.dot(row_mats[0], chosen, preferred_element_type=jnp.float32)
    outputs = [product.astype(jnp.bfloat16)]
    return jnp.stack(outputs, 0)


def body(
    fine_waves,
    coarse_waves,
    coarse_kernel,
    row_valence,
    row_conduction,
    row_neighbours,
    row_weight_index,
    col_neighbours,
    col_weight_index,
    tile_list,
    weight_table,
):
    owner_count = lax.axis_size("ka")
    owner_index = lax.axis_index("ka")
    fine_count, band_count, wave_count = fine_waves.shape
    held_cols = coarse_waves.shape[0]
    rows_here = row_valence.shape[0]
    departure, arrival = slot_tables(tile_list, owner_index, held_cols, SLOT_COUNT)
    picked = jnp.take(coarse_waves, departure, axis=0).reshape(
        owner_count, SLOT_COUNT, band_count, wave_count
    )
    arrived = lax.all_to_all(picked, "ka", split_axis=0, concat_axis=0, tiled=True)
    list_waves = jnp.take(
        arrived.reshape(owner_count * SLOT_COUNT, band_count, wave_count), arrival, axis=0
    )
    valence_part = band_correlations(
        fine_waves[:, :VALENCE], list_waves[:, :VALENCE], col_neighbours
    )
    conduction_part = band_correlations(
        fine_waves[:, VALENCE:], list_waves[:, VALENCE:], col_neighbours
    )
    valence_sum, conduction_sum = in_one((valence_part, conduction_part), "ga")
    inv_root = 1.0 / math.sqrt(PLANE_WAVES)
    col_rotation = pair_tiles(
        table_lookup(col_weight_index, weight_table),
        valence_sum * inv_root,
        conduction_sum * inv_root,
    )
    row_rotation = pair_tiles(
        table_lookup(row_weight_index, weight_table), row_valence, row_conduction
    )
    row_mats = jnp.transpose(row_rotation, (0, 2, 1, 3)).reshape(
        rows_here, BAND_PAIRS, CORNERS * BAND_PAIRS
    )
    upper = passed_along(coarse_kernel, "ga", -1)
    rotated = rotate_rows(jnp.concatenate([coarse_kernel, upper], 0), row_mats, row_neighbours)
    rotated = rotated.reshape(rows_here, BAND_PAIRS, held_cols, BAND_PAIRS)
    outgoing = jnp.take(rotated, departure, axis=2).reshape(
        rows_here, BAND_PAIRS, owner_count, SLOT_COUNT * BAND_PAIRS
    )
    incoming = lax.all_to_all(outgoing, "ka", split_axis=2, concat_axis=2, tiled=True)
    incoming = incoming.reshape(rows_here, BAND_PAIRS, owner_count * SLOT_COUNT, BAND_PAIRS)
    left_tiles = jnp.take(incoming, arrival, axis=2)
    gathered = jnp.take(left_tiles, col_neighbours, axis=2)
    result = jnp.einsum(
        "rafjb,fjcb->rfac", gathered, col_rotation, preferred_element_type=jnp.float32
    )
    return result.reshape(rows_here, fine_count, BAND_PAIRS * BAND_PAIRS).astype(jnp.bfloat16)


def solution(mesh):
    placed = (
        P("ka", None, "ga"),
        P("ka", None, "ga"),
        P("ga", None, "ka"),
        P("ga", None, None, None),
        P("ga", None, None, None),
        P("ga", None),
        P("ga", None),
        P("ka", None),
        P("ka", None),
        P(),
        P(),
    )
    return jax.shard_map(
        body, mesh=mesh, in_specs=placed, out_specs=P("ga", "ka", None), check_vma=False
    )
```

profile of v0, /device:TPU:1, one launch (start us, length us, event | category | flops | bytes accessed | tf_op | source)
XLA Modules:
  0.0 379.8 jit_solution(16632348271607740939)
XLA Ops:
  0.0 0.8 broadcast_compare_fusion.1
  0.8 0.7 broadcast_subtract_fusion
  1.5 0.5 convert_reduce_fusion
  1.9 0.2 select_reduce_fusion
  2.3 0.1 copy.91
  2.4 0.7 gather_fusion
  3.2 1.8 broadcast_select_fusion
  5.0 15.9 %all-to-all-start = ((bf16[16,4,16,1280]{3,2,1,0:T(8,128)(2,1)}), bf16[16,4,16,1280]{3,2,1,0:T(8,128)(2,1)}, u32[]{:S(2)}, u32[]{:S(2)}) async-start(bf16[16,4,16,1280]{3,2,1,0:T(8,128)(2,1)} %broadcast_select_fusion), calls=%async_computation | async-start | bytes 5242880 | tf_op jit(solution)/shard_map/all_to_all | solution.py:119
  20.9 2.9 collective-permute-start
  23.9 0.3 broadcast_multiply_fusion.1
  24.2 0.6 mul.130
  24.8 0.2 select_reduce_fusion.2
  25.1 0.1 fusion.23
  25.2 0.1 fusion.16
  25.3 0.3 reshape.499
  25.6 0.1 squeeze_reshape.3
  26.0 4.8 %collective-permute-done = bf16[6,64,512]{2,1,0:T(8,128)(2,1)S(1)} collective-permute-done((bf16[6,64,512]{2,1,0:T(8,128)(2,1)S(1)}, bf16[6,64,512]{2,1,0:T(8,128)(2,1)S(1)}, u32[]{:S(2)}, u32[]{:S(2)}) %collective-permute-start) | collective-permute-done | bytes 393248 | tf_op jit(solution)/shard_map/ppermute | solution.py:38
  30.8 0.6 gather_fusion.2
  31.4 0.1 broadcast_select_fusion.2
  31.5 0.2 convolution_convert_fusion
  31.8 0.1 reshape.452
  31.9 0.7 gather_fusion.3
  32.7 0.7 copy.105
  33.4 0.7 gather.38
  34.1 1.0 copy.106
  35.1 100.3 %all-to-all-done = bf16[16,4,16,1280]{3,2,1,0:T(8,128)(2,1)} async-done(((bf16[16,4,16,1280]{3,2,1,0:T(8,128)(2,1)}), bf16[16,4,16,1280]{3,2,1,0:T(8,128)(2,1)}, u32[]{:S(2)}, u32[]{:S(2)}) %all-to-all-start) | async-done | bytes 2621472 | tf_op jit(solution)/shard_map/all_to_all | solution.py:119
  135.4 11.2 %all-to-all-start.2 = ((bf16[1,64,16,256]{3,1,0,2:T(8,128)(2,1)}), bf16[1,64,16,256]{3,1,0,2:T(8,128)(2,1)}, u32[]{:S(2)}, u32[]{:S(2)}) async-start(bf16[1,64,16,256]{3,1,0,2:T(8,128)(2,1)} %copy.106), calls=%async_computation.2 | async-start | bytes 1048576 | tf_op jit(solution)/shard_map/all_to_all | solution.py:148
  146.6 2.4 gather_fusion.1
  149.0 0.2 broadcast_select_fusion.1
  149.2 1.1 copy-done.3
  150.3 0.3 convolution_bitcast_fusion
  150.6 0.1 copy.95
  150.7 1.1 reshape.412
  151.9 81.1 %gather_fusion.7 = f32[8192]{0:T(1024)S(1)} fusion(f32[16,8,32,8]{3,2,1,0:T(8,128)S(1)} %reshape.412, s32[8192]{0:T(1024)S(1)} %reshape.499), kind=kCustom, calls=%fused_computation.1.clone | custom fusion | bytes 196608 | tf_op jit(solution)/shard_map/jit(take_along_axis)/gather | solution.py:86
  232.9 1.1 reshape.507
  234.0 1.4 convolution_bitcast_fusion.1
  235.6 1.1 reshape.408
  236.7 81.1 %gather_fusion.6 = f32[8192]{0:T(1024)S(1)} fusion(f32[16,8,32,8]{3,2,1,0:T(8,128)S(1)} %reshape.408, s32[8192]{0:T(1024)S(1)} %reshape.499), kind=kCustom, calls=%fused_computation.clone | custom fusion | bytes 196608 | tf_op jit(solution)/shard_map/jit(take_along_axis)/gather | solution.py:86
  317.8 0.3 reshape.502
  318.2 0.1 select_bitcast_fusion.1
  318.3 0.1 copy.94
  318.4 0.3 reshape.409
  318.7 0.1 copy.96
  318.8 0.3 reshape.413
  319.1 3.2 broadcast_in_dim.141
  322.3 8.0 %all-to-all-start.1 = ((f32[32,1,16384]{2,1,0:T(1,128)}), f32[32,1,16384]{2,1,0:T(1,128)S(1)}, u32[]{:S(2)}, u32[]{:S(2)}) async-start(f32[32,1,16384]{2,1,0:T(1,128)} %broadcast_in_dim.141), calls=%async_computation.1 | async-start | bytes 4194304 | tf_op jit(solution)/shard_map/all_to_all | solution.py:17
  330.7 2.1 copy.107
  332.8 1.6 reshape.462
  334.5 1.7 copy.108
  336.1 2.0 gather_fusion.4
  338.1 0.1 fusion.17
  338.2 2.2 gather_fusion.5
  340.4 18.4 %all-to-all-done.1 = f32[32,1,16384]{2,1,0:T(1,128)S(1)} async-done(((f32[32,1,16384]{2,1,0:T(1,128)}), f32[32,1,16384]{2,1,0:T(1,128)S(1)}, u32[]{:S(2)}, u32[]{:S(2)}) %all-to-all-start.1) | async-done | bytes 2097184 | tf_op jit(solution)/shard_map/all_to_all | solution.py:17
  358.8 1.4 reduce_sum.48
  360.2 0.3 mul.116
  360.5 0.3 copy.98
  360.8 0.3 mul.119
  361.1 0.3 copy.99
  361.4 2.3 broadcast_multiply_fusion
  363.8 4.6 %multiply_convert_fusion = bf16[16,8,64,64]{0,3,2,1:T(8,128)(2,1)} fusion(f32[16,8,64,64]{0,3,2,1:T(8,128)S(1)} %bitcast.99, f32[16,8]{0,1:T(8,128)S(1)} %select_reduce_fusion.1), kind=kLoop, calls=%fused_computation.8 | loop fusion | flops 1572864 | bytes 3146240 | tf_op jit(solution)/shard_map/convert_element_type | solution.py:51
  368.4 8.0 %copy.110 = bf16[16,8,64,64]{3,2,1,0:T(8,128)(2,1)S(1)} copy(bf16[16,8,64,64]{0,3,2,1:T(8,128)(2,1)} %multiply_convert_fusion) | data formatting | bytes 2097152 | tf_op jit(solution)/shard_map/convert_element_type | solution.py:51
  376.3 2.4 fusion.10
  378.7 0.2 copy.111
  378.9 0.9 convert_element_type.47
  (82 shorter events, 1.3 us)
Async XLA Ops:
  0.0 2.4 copy-start
  3.1 17.8 %copy-start.4 = (bf16[6,64,512]{2,1,0:T(8,128)(2,1)S(1)}, bf16[6,64,512]{2,1,0:T(8,128)(2,1)}, u32[]{:S(2)}) copy-start(bf16[6,64,512]{2,1,0:T(8,128)(2,1)} %param.15) | copy-start | bytes 1179652
  3.1 20.7 %copy-start.9 = (s32[16,8]{0,1:T(8,128)S(1)}, s32[16,8]{0,1:T(8,128)}, u32[]{:S(2)}) copy-start(s32[16,8]{0,1:T(8,128)} %param.20) | copy-start | bytes 1540
  3.1 20.7 %copy-start.11 = (f32[1,8,8,8]{3,2,1,0:T(8,128)S(1)}, f32[1,8,8,8]{3,2,1,0:T(8,128)}, u32[]{:S(2)}) copy-start(f32[1,8,8,8]{3,2,1,0:T(8,128)} %param.16) | copy-start | bytes 6148
  3.2 20.7 %copy-start.12 = (f32[1,8,8,8]{3,2,1,0:T(8,128)S(1)}, f32[1,8,8,8]{3,2,1,0:T(8,128)}, u32[]{:S(2)}) copy-start(f32[1,8,8,8]{3,2,1,0:T(8,128)} %param.17) | copy-start | bytes 6148
  5.0 19.8 %copy-start.19 = (f32[8]{0:T(128)S(1)}, f32[8]{0:T(128)}, u32[]{:S(2)}) copy-start(f32[8]{0:T(128)} %param.23) | copy-start | bytes 100
  5.0 19.8 %copy-start.23 = (s32[1,8]{1,0:T(1,128)S(1)}, s32[1,8]{1,0:T(1,128)}, u32[]{:S(2)}) copy-start(s32[1,8]{1,0:T(1,128)} %param.19) | copy-start | bytes 100
  5.0 20.3 %copy-start.24 = (s32[1,8]{1,0:T(1,128)S(1)}, s32[1,8]{1,0:T(1,128)}, u32[]{:S(2)}) copy-start(s32[1,8]{1,0:T(1,128)} %param.18) | copy-start | bytes 100
  5.0 130.4 %all-to-all-start = ((bf16[16,4,16,1280]{3,2,1,0:T(8,128)(2,1)}), bf16[16,4,16,1280]{3,2,1,0:T(8,128)(2,1)}, u32[]{:S(2)}, u32[]{:S(2)}) async-start(bf16[16,4,16,1280]{3,2,1,0:T(8,128)(2,1)} %broadcast_select_fusion), calls=%async_computation | async-start | bytes 5242880 | tf_op jit(solution)/shard_map/all_to_all | solution.py:119
  20.9 9.8 %collective-permute-start = (bf16[6,64,512]{2,1,0:T(8,128)(2,1)S(1)}, bf16[6,64,512]{2,1,0:T(8,128)(2,1)S(1)}, u32[]{:S(2)}, u32[]{:S(2)}) collective-permute-start(bf16[6,64,512]{2,1,0:T(8,128)(2,1)S(1)} %copy-done.4), channel_id=1, source_target_pairs={{0,496},{16,0},{32,16},{48,32},{64,48},{80,64},{96,80},{112,96},{1... | collective-permute-start | bytes 1179656 | tf_op jit(solution)/shard_map/ppermute | solution.py:38
  23.9 7.5 %copy-start.5 = (s32[16,8]{1,0:T(8,128)}, s32[16,8]{1,0:T(8,128)S(1)}, u32[]{:S(2)}) copy-start(s32[16,8]{1,0:T(8,128)S(1)} %copy.90) | copy-start | bytes 1540
  25.0 0.6 copy-start.13
  25.0 6.5 %copy-start.7 = (s32[16,8]{1,0:T(8,128)}, s32[16,8]{1,0:T(8,128)S(1)}, u32[]{:S(2)}) copy-start(s32[16,8]{1,0:T(8,128)S(1)} %broadcast_add_fusion) | copy-start | bytes 1540
  34.0 116.2 %copy-start.21 = (bf16[16,16,1280]{2,1,0:T(8,128)(2,1)S(1)}, bf16[16,16,1280]{2,1,0:T(8,128)(2,1)}, u32[]{:S(2)}) copy-start(bf16[16,16,1280]{2,1,0:T(8,128)(2,1)} %param.13) | copy-start | bytes 1966084
  135.4 183.7 %all-to-all-start.2 = ((bf16[1,64,16,256]{3,1,0,2:T(8,128)(2,1)}), bf16[1,64,16,256]{3,1,0,2:T(8,128)(2,1)}, u32[]{:S(2)}, u32[]{:S(2)}) async-start(bf16[1,64,16,256]{3,1,0,2:T(8,128)(2,1)} %copy.106), calls=%async_computation.2 | async-start | bytes 1048576 | tf_op jit(solution)/shard_map/all_to_all | solution.py:148
  146.5 2.6 copy-start.16
  146.6 2.6 copy-start.15
  149.2 1.1 copy-start.3
  151.8 82.2 %copy-start.22 = (bf16[16,16,1280]{2,1,0:T(8,128)(2,1)S(1)}, bf16[16,16,1280]{2,1,0:T(8,128)(2,1)}, u32[]{:S(2)}) copy-start(bf16[16,16,1280]{2,1,0:T(8,128)(2,1)} %param.13) | copy-start | bytes 1966084
  236.7 81.4 %copy-start.2 = (f32[16,8,8,8]{3,2,1,0:T(8,128)S(1)}, f32[16,8,8,8]{3,2,1,0:T(8,128)}, u32[]{:S(2)}) copy-start(f32[16,8,8,8]{3,2,1,0:T(8,128)} %reshape.507) | copy-start | bytes 98308
  236.7 81.4 %copy-start.6 = (s32[16,8]{1,0:T(8,128)S(1)}, s32[16,8]{1,0:T(8,128)}, u32[]{:S(2)}) copy-start(s32[16,8]{1,0:T(8,128)} %copy-done.5) | copy-start | bytes 1540
  236.7 81.4 %copy-start.8 = (s32[16,8]{1,0:T(8,128)S(1)}, s32[16,8]{1,0:T(8,128)}, u32[]{:S(2)}) copy-start(s32[16,8]{1,0:T(8,128)} %copy-done.7) | copy-start | bytes 1540
  236.7 81.4 %copy-start.14 = (pred[16,8]{1,0:T(8,128)(4,1)S(1)}, pred[16,8]{1,0:T(8,128)(4,1)}, u32[]{:S(2)}) copy-start(pred[16,8]{1,0:T(8,128)(4,1)} %copy-done.13) | copy-start | bytes 388
  318.4 11.9 %copy-start.10 = (s32[16,8]{0,1:T(8,128)S(1)}, s32[16,8]{0,1:T(8,128)}, u32[]{:S(2)}) copy-start(s32[16,8]{0,1:T(8,128)} %param.20) | copy-start | bytes 1540
  318.7 11.9 %copy-start.18 = (s32[16,8]{0,1:T(8,128)S(1)}, s32[16,8]{0,1:T(8,128)}, u32[]{:S(2)}) copy-start(s32[16,8]{0,1:T(8,128)} %param.21) | copy-start | bytes 1540
  318.7 11.9 %copy-start.20 = (f32[8]{0:T(128)S(1)}, f32[8]{0:T(128)}, u32[]{:S(2)}) copy-start(f32[8]{0:T(128)} %param.23) | copy-start | bytes 100
  322.3 15.8 %copy-start.17 = (pred[32]{0:T(512)(128)(4,1)S(1)}, pred[32]{0:T(512)(128)(4,1)}, u32[]{:S(2)}) copy-start(pred[32]{0:T(512)(128)(4,1)} %copy-done.16) | copy-start | bytes 100
  322.3 36.5 %all-to-all-start.1 = ((f32[32,1,16384]{2,1,0:T(1,128)}), f32[32,1,16384]{2,1,0:T(1,128)S(1)}, u32[]{:S(2)}, u32[]{:S(2)}) async-start(f32[32,1,16384]{2,1,0:T(1,128)} %broadcast_in_dim.141), calls=%async_computation.1 | async-start | bytes 4194304 | tf_op jit(solution)/shard_map/all_to_all | solution.py:17
  368.4 11.5 %copy-start.1 = (bf16[8,16,1280]{2,1,0:T(8,128)(2,1)S(1)}, bf16[8,16,1280]{2,1,0:T(8,128)(2,1)}, u32[]{:S(2)}) copy-start(bf16[8,16,1280]{2,1,0:T(8,128)(2,1)} %param.14) | copy-start | bytes 983044
where the time goes:
time: 381 us; the launch traced here: 380 us
  local copies, waits for them, and re-layouts  200 us (52%)
  waiting for transfers between devices  123 us (32%)
  starting transfers between devices  37.9 us (10%)
  other arithmetic  13.8 us (4%)
  matrix products  4.3 us (1%)
    gather x5, local copies, waits for them, and re-layouts, band_correlations(): chosen = jnp.take_along_axis(dense, picks, axis=2)  164 us
    all_to_all x1, waiting for transfers between devices, body(): lax.all_to_all(picked, 'ka', split_axis=0, concat_axis=0, tiled=True)  100 us
    all_to_all x1, waiting for transfers between devices, sent_to_all(): lax.all_to_all(jnp.broadcast_to(array[None], (peers, *array.shape)), axis...  18.4 us
    all_to_all x1, starting transfers between devices, body(): lax.all_to_all(picked, 'ka', split_axis=0, concat_axis=0, tiled=True)  15.9 us
    all_to_all x1, starting transfers between devices, body(): lax.all_to_all(outgoing, 'ka', split_axis=2, concat_axis=2, tiled=True)  11.2 us
    all_to_all x1, starting transfers between devices, sent_to_all(): lax.all_to_all(jnp.broadcast_to(array[None], (peers, *array.shape)), axis...  8 us
    convert_element_type x1, local copies, waits for them, and re-layouts, pair_tiles(): return scaled.astype(jnp.bfloat16)  7.98 us
  transfers between devices with their start and end apart: 4, of which 3 were waited for; matrix products, arithmetic and copies ran while one was open for 49% of the time, Pallas kernels for 0%

commit v1 on v0

v1 whole, which is shorter than its diff:
```python
import functools
import math

import jax
import jax.numpy as jnp
from jax import lax
from jax.experimental import pallas as pl
from jax.experimental.pallas import tpu as pltpu
from jax.sharding import PartitionSpec as P

MESH = pl.DeviceIdType.MESH
PLANE_WAVES = 40960
CORNERS = 8
PAIRS = 64
BANDS = 16
F32 = jnp.float32
BF16 = jnp.bfloat16
LAG = 2


def lanes(shape):
    return lax.broadcasted_iota(jnp.int32, shape, len(shape) - 1)


def kernel(
    nz, row_peers, line_peers,
    fine_hbm, coarse_hbm, tiles_hbm, rv, rc, rn, rwi, cn, cwi, tl, wt,
    out,
    fine, waves, dense, stack, left, spread, expanded, rsm, mixed, sel, from_row, sum1,
    from_line, sum2, full, off_d, off_l, wgt,
    in_sem, ws, wr, up_s, up_r, ts, tr, rs_s, rs_r, ln_s, ln_r, ag_s, ag_r,
):
    g, z = lax.axis_index("ga"), lax.axis_index("ka")
    ng = row_peers * line_peers
    half = nz // 2
    col_rows = waves.shape[1] // 2
    y, j_me = g // row_peers, lax.rem(g, row_peers)
    nbr = (lax.rem(z + 1, nz), lax.rem(z + nz - 1, nz))

    get_coarse = pltpu.make_async_copy(coarse_hbm, waves.at[0], in_sem.at[0])
    get_tiles = pltpu.make_async_copy(tiles_hbm, stack.at[pl.ds(0, 6)], in_sem.at[1])
    get_fine = pltpu.make_async_copy(fine_hbm, fine, in_sem.at[2])
    get_coarse.start()
    get_tiles.start()
    get_fine.start()

    def row_peer(r):
        return y * row_peers + lax.rem(j_me + r, row_peers)

    def line_peer(r):
        return lax.rem(y + r, line_peers) * row_peers + j_me

    up_to, up_from = lax.rem(g + ng - 1, ng), lax.rem(g + 1, ng)
    barrier = pltpu.get_barrier_semaphore()
    friends = [(g, nbr[0]), (g, nbr[1]), (up_to, z), (up_from, z)]
    friends += [(row_peer(r), z) for r in range(1, row_peers)]
    friends += [(line_peer(r), z) for r in range(1, line_peers)]
    for who in friends:
        pl.semaphore_signal(barrier, inc=1, device_id=who, device_id_type=MESH)
    pl.semaphore_wait(barrier, len(friends))

    def slot(way, d):
        return lax.rem(nz - d, nz) if way == 0 else d

    def wave(way, d, j):
        rows = pl.ds(j * col_rows, col_rows)
        return pltpu.make_async_remote_copy(
            src_ref=waves.at[slot(way, d - 1), rows],
            dst_ref=waves.at[slot(way, d), rows],
            send_sem=ws.at[way, d - 1, j],
            recv_sem=wr.at[way, d - 1, j],
            device_id=(g, nbr[way]),
            device_id_type=MESH,
        )

    def tile(way, k, part=None):
        first, count = (0, 4) if part is None else (part * 2, 2)
        return pltpu.make_async_remote_copy(
            src_ref=left.at[pl.ds(slot(way, k - 1) * 4 + first, count)],
            dst_ref=left.at[pl.ds(slot(way, k) * 4 + first, count)],
            send_sem=ts.at[way, k - 1],
            recv_sem=tr.at[way, k - 1],
            device_id=(g, nbr[way]),
            device_id_type=MESH,
        )

    def swap(base, count):
        for q in range(count):
            v = left[base + q].astype(F32)
            left[nz * 4 + base + q] = pltpu.roll(v, 64, 1).astype(BF16)

    def correlate(s, j):
        part = waves[s, pl.ds(j * col_rows, col_rows), :]
        at = (s * (2 * col_rows) + j * col_rows) // 8
        both = lax.dot_general(
            part, fine[...], (((1,), (1,)), ((), ())), preferred_element_type=F32
        )
        dense[pl.ds(at, col_rows // 8)] = both.reshape(col_rows // 8, 8, 256)

    get_coarse.wait()
    for jj in range(2):
        wave(0, 1, jj).start()
        wave(1, 1, 1 - jj).start()
    get_tiles.wait()
    upper = pltpu.make_async_remote_copy(
        src_ref=stack.at[pl.ds(0, 6)],
        dst_ref=stack.at[pl.ds(6, 6)],
        send_sem=up_s,
        recv_sem=up_r,
        device_id=(up_to, z),
        device_id_type=MESH,
    )
    upper.start()
    get_fine.wait()
    for j in range(2):
        correlate(0, j)

    scale = 1.0 / (PLANE_WAVES * math.sqrt(PAIRS))

    def place(i, carry):
        f, c = i // CORNERS, i % CORNERS
        col = tl[z, cn[f, c]]
        s = (lax.shift_right_logical(col, 3) - z + nz) & (nz - 1)
        jj = col & 7
        off_d[i] = (s * 8 + jj) * 2
        off_l[i] = s * 4 + lax.shift_right_logical(jj, 1) + ((jj + c) & 1) * (nz * 4)
        wgt[i] = wt[cwi[f, c]] * scale
        return carry

    lax.fori_loop(0, 128, place, 0)

    into = lanes((128, 1024))
    row = lax.broadcasted_iota(jnp.int32, (128, 1024), 0)
    local = into % 512
    wanted = (local // 64) * 16 + jnp.where(into < 512, (local % 64) // 8, 8 + local % 8)
    spread[...] = jnp.where(row == wanted, 1.0, 0.0).astype(BF16)

    def wave_step(d):
        for jj in range(2):
            for way in range(2):
                j = jj if way == 0 else 1 - jj
                wave(way, d, j).wait_recv()
                if jj == 0:
                    wave(way, d + 1, j).start()
                else:

                    @pl.when(d < half - 1)
                    def _():
                        wave(way, d + 1, j).start()

                correlate(slot(way, d), j)

    wave_step(1)

    wide = lanes((8, PAIRS))
    low = lax.broadcasted_iota(jnp.int32, (8, PAIRS), 0)
    to_w = jnp.where(wide // 8 == low, 1.0, 0.0)
    to_y = jnp.where(wide % 8 == low, 1.0, 0.0)
    exact = lax.Precision.HIGHEST
    row_v = jnp.dot(rv[...], to_w, precision=exact, preferred_element_type=F32)
    row_c = jnp.dot(rc[...], to_y, precision=exact, preferred_element_type=F32)
    upper.wait_recv()
    rotated = jnp.zeros((PAIRS, stack.shape[2]), F32)
    for c in range(CORNERS):
        w = wt[rwi[0, c]]
        cond = row_c[c * 8 : c * 8 + 8]
        mat = jnp.concatenate(
            [row_v[c * 8 + v : c * 8 + v + 1] * cond for v in range(8)], axis=0
        )
        mat = (w * mat * (1.0 / math.sqrt(PAIRS))).astype(BF16)
        rotated += jnp.dot(mat, stack[rn[0, c]], preferred_element_type=F32)
    rotated = rotated.astype(BF16)
    for q in range(4):
        left[q] = rotated[:, q * 128 : (q + 1) * 128]
    swap(0, 4)

    def tile_step(k, parts=False):
        for way in range(2):
            tile(way, k).wait_recv()
        for way in range(2):
            tile(way, k + 1, way if parts else None).start()
        for way in range(2):
            swap(slot(way, k) * 4, 4)

    def both(d, carry):
        wave_step(d)

        @pl.when(d == 1 + LAG)
        def _():
            for way in range(2):
                tile(way, 1).start()

        @pl.when(d > 1 + LAG)
        def _():
            tile_step(d - 1 - LAG)

        return carry

    lax.fori_loop(2, half, both, 0)
    for way in range(2):
        wave(way, half, way).wait_recv()
        correlate(half, way)

    lane = lanes((8, 128))

    def pick(c, carry):
        for t in range(2):
            acc = jnp.zeros((8, 128), F32)
            for ff in range(8):
                i = (t * 8 + ff) * CORNERS + c
                val = dense[off_d[i], :, t * 128 : t * 128 + 128] * wgt[i]
                cond = dense[off_d[i] + 1, :, t * 128 : t * 128 + 128]
                acc = jnp.where(lane // 8 == 2 * ff, val, acc)
                acc = jnp.where(lane // 8 == 2 * ff + 1, cond, acc)
            sel[c, :, pl.ds(t * 128, 128)] = acc
        return carry

    lax.fori_loop(0, CORNERS, pick, 0)

    def to_row(r):
        return pltpu.make_async_remote_copy(
            src_ref=sel.at[lax.rem(j_me + r, row_peers)],
            dst_ref=from_row.at[r - 1],
            send_sem=rs_s.at[r - 1],
            recv_sem=rs_r.at[r - 1],
            device_id=(row_peer(r), z),
            device_id_type=MESH,
        )

    def to_line(r):
        return pltpu.make_async_remote_copy(
            src_ref=sum1,
            dst_ref=from_line.at[r - 1],
            send_sem=ln_s.at[r - 1],
            recv_sem=ln_r.at[r - 1],
            device_id=(line_peer(r), z),
            device_id_type=MESH,
        )

    def to_all(r):
        return pltpu.make_async_remote_copy(
            src_ref=sum2,
            dst_ref=full.at[j_me],
            send_sem=ag_s.at[r - 1],
            recv_sem=ag_r.at[r - 1],
            device_id=(row_peer(r), z),
            device_id_type=MESH,
        )

    def got_all(r):
        return pltpu.make_async_remote_copy(
            src_ref=sum2,
            dst_ref=full.at[lax.rem(j_me + row_peers - r, row_peers)],
            send_sem=ag_s.at[r - 1],
            recv_sem=ag_r.at[r - 1],
            device_id=(row_peer(r), z),
            device_id_type=MESH,
        )

    for r in range(1, row_peers):
        to_row(r).start()
    first_late = half - 1 - LAG
    tile_step(first_late)
    total = sel[j_me]
    for r in range(1, row_peers):
        to_row(r).wait_recv()
        total += from_row[r - 1]
    sum1[...] = total
    for r in range(1, line_peers):
        to_line(r).start()
    tile_step(first_late + 1)
    for r in range(1, line_peers):
        to_line(r).wait_recv()
        total += from_line[r - 1]
    sum2[...] = total
    full[j_me] = total
    for r in range(1, row_peers):
        to_all(r).start()
    tile_step(first_late + 2, parts=True)
    for r in range(1, row_peers):
        got_all(r).wait_recv()

    corr = full[...].reshape(CORNERS * 8, 256)
    corr = jnp.concatenate([corr[:, :128], corr[:, 128:]], axis=0)
    high = corr.astype(BF16)
    rest = (corr - high.astype(F32)).astype(BF16)
    expanded[...] = jnp.dot(high, spread[...], preferred_element_type=F32) + jnp.dot(
        rest, spread[...], preferred_element_type=F32
    )

    def rotate(c, carry):
        for t in range(2):
            at = pl.multiple_of(t * 64 + c * 8, 8)
            val = expanded[pl.ds(at, 8), pl.ds(0, 512)]
            cond = expanded[pl.ds(at, 8), pl.ds(512, 512)]
            for w in range(0, 8, 2):
                both_w = jnp.concatenate([val[w : w + 1] * cond, val[w + 1 : w + 2] * cond], 0)
                to = pl.multiple_of(c * 64 + w * 8, 16)
                rsm[pl.ds(to, 16), pl.ds(t * 512, 512)] = both_w.astype(BF16)
        return carry

    lax.fori_loop(0, CORNERS, rotate, 0)

    for way in range(2):
        tile(way, half, way).wait_recv()
    swap(half * 4, 4)

    near = lanes((64, 128)) < 64

    for p in range(8):
        blocks = []
        for ff in range(2):
            f = p * 2 + ff
            quads = []
            for q in range(4):
                a = left[off_l[f * CORNERS + 2 * q]]
                b = left[off_l[f * CORNERS + 2 * q + 1]]
                quads.append(jnp.where(near, a, b))
            blocks.append(jnp.concatenate(quads, axis=1))
        res = jnp.dot(
            jnp.concatenate(blocks, axis=0),
            rsm[:, p * 128 : (p + 1) * 128],
            preferred_element_type=F32,
        )
        turned = pltpu.roll(res, 64, 1)
        mixed[p * 128 : p * 128 + 64, :] = jnp.where(near, res[:64], turned[:64])
        mixed[p * 128 + 64 : p * 128 + 128, :] = jnp.where(near, turned[64:], res[64:])

    near_f = lanes((16, 128)) < 64
    for t in range(32):
        even = mixed[pl.ds(2 * t, 16, stride=64), :]
        odd = mixed[pl.ds(2 * t + 1, 16, stride=64), :]
        out[:, t * 128 : (t + 1) * 128] = jnp.where(near_f, even, odd).astype(BF16)

    upper.wait_send()

    def sent(d, carry):
        for way in range(2):
            for j in range(2):
                wave(way, d, j).wait_send()
            tile(way, d).wait_send()
        return carry

    lax.fori_loop(1, half, sent, 0)
    for way in range(2):
        wave(way, half, way).wait_send()
        tile(way, half, way).wait_send()
    for r in range(1, row_peers):
        to_row(r).wait_send()
        to_all(r).wait_send()
    for r in range(1, line_peers):
        to_line(r).wait_send()


def body(mesh_shape, *args):
    (fine_waves, coarse_waves, coarse_kernel, row_valence, row_conduction, row_neighbours,
     row_weight_index, col_neighbours, col_weight_index, tile_list, weight_table) = args
    nz, ng = mesh_shape
    row_peers, line_peers = CORNERS, ng // CORNERS
    width = fine_waves.shape[2]
    held = coarse_waves.shape[0] * BANDS
    any_space = pl.BlockSpec(memory_space=pl.ANY)
    vmem = pl.BlockSpec(memory_space=pltpu.VMEM)
    smem = pl.BlockSpec(memory_space=pltpu.SMEM)
    half = nz // 2
    dma = pltpu.SemaphoreType.DMA
    out = pl.pallas_call(
        functools.partial(kernel, nz, row_peers, line_peers),
        out_shape=jax.ShapeDtypeStruct((16, PAIRS * PAIRS), BF16),
        in_specs=[any_space] * 3 + [vmem] * 2 + [smem] * 6,
        out_specs=vmem,
        scratch_shapes=[
            pltpu.VMEM((256, width), BF16),
            pltpu.VMEM((nz, held, width), BF16),
            pltpu.VMEM((nz * held // 8, 8, 256), F32),
            pltpu.VMEM((12, PAIRS, 512), BF16),
            pltpu.VMEM((2 * nz * 4, PAIRS, 128), BF16),
            pltpu.VMEM((128, 1024), BF16),
            pltpu.VMEM((128, 1024), F32),
            pltpu.VMEM((512, 1024), BF16),
            pltpu.VMEM((1024, 128), F32),
            pltpu.VMEM((CORNERS, 8, 256), F32),
            pltpu.VMEM((row_peers - 1, 8, 256), F32),
            pltpu.VMEM((8, 256), F32),
            pltpu.VMEM((line_peers - 1, 8, 256), F32),
            pltpu.VMEM((8, 256), F32),
            pltpu.VMEM((CORNERS, 8, 256), F32),
            pltpu.SMEM((128,), jnp.int32),
            pltpu.SMEM((128,), jnp.int32),
            pltpu.SMEM((128,), F32),
            dma((3,)),
            dma((2, half, 2)),
            dma((2, half, 2)),
            dma,
            dma,
            dma((2, half)),
            dma((2, half)),
            dma((row_peers - 1,)),
            dma((row_peers - 1,)),
            dma((line_peers - 1,)),
            dma((line_peers - 1,)),
            dma((row_peers - 1,)),
            dma((row_peers - 1,)),
        ],
        compiler_params=pltpu.CompilerParams(
            collective_id=0, has_side_effects=True, vmem_limit_bytes=40 * 1024 * 1024
        ),
        name="interpolate",
    )(
        fine_waves.reshape(16 * BANDS, width),
        coarse_waves.reshape(held, width),
        coarse_kernel,
        row_valence.reshape(64, 8),
        row_conduction.reshape(64, 8),
        row_neighbours,
        row_weight_index,
        col_neighbours,
        col_weight_index,
        tile_list,
        weight_table,
    )
    return out[None]


def solution(mesh):
    placed = (
        P("ka", None, "ga"),
        P("ka", None, "ga"),
        P("ga", None, "ka"),
        P("ga", None, None, None),
        P("ga", None, None, None),
        P("ga", None),
        P("ga", None),
        P("ka", None),
        P("ka", None),
        P(),
        P(),
    )
    shape = (mesh.shape["ka"], mesh.shape["ga"])
    return jax.shard_map(
        functools.partial(body, shape),
        mesh=mesh,
        in_specs=placed,
        out_specs=P("ga", "ka", None),
        check_vma=False,
    )
```

time: 381 us -> 99.5 us (0.26)
  local copies, waits for them, and re-layouts: 200 us -> 7.29 us
  waiting for transfers between devices: 123 us -> 0 us
  Pallas kernels: 0 us -> 91.7 us
  starting transfers between devices: 37.9 us -> 0 us
  other arithmetic: 13.8 us -> 0 us
  matrix products: 4.3 us -> 0 us
    gather x13 -> x0, local copies, waits for them, and re-layouts: 174 us -> none  [the longest x5 164 us: band_correlations(): chosen = jnp.take_along_axis(dense, picks, axis=2)]
    all_to_all x3 -> x0, waiting for transfers between devices: 119 us -> none  [the longest x1 100 us: body(): lax.all_to_all(picked, 'ka', split_axis=0, concat_axis=0, tiled=True)]
    pallas_call x0 -> x1, Pallas kernels: none -> 91.7 us  [body(): pl.pallas_call(functools.partial(kernel, nz, row_peers, line_peers), out_...]
    all_to_all x3 -> x0, starting transfers between devices: 35.1 us -> none  [the longest x1 15.9 us: body(): lax.all_to_all(picked, 'ka', split_axis=0, concat_axis=0, tiled=True)]
    convert_element_type x3 -> x0, local copies, waits for them, and re-layouts: 9.09 us -> none  [the longest x1 7.98 us: pair_tiles(): return scaled.astype(jnp.bfloat16)]
    reshape x7 -> x0, local copies, waits for them, and re-layouts: 6.14 us -> none  [the longest x2 3.27 us: body(): incoming.reshape(rows_here, BAND_PAIRS, owner_count * SLOT_COUNT, BAND_PA...]
    unnamed x51 -> x25, local copies, waits for them, and re-layouts: 1.29 us -> 7.29 us
    ppermute x1 -> x0, waiting for transfers between devices: 4.79 us -> none  [passed_along(): lax.ppermute(array, axis, [(i, (i + by) % peers) for i in range(peers)])]
  transfers between devices with their start and end apart: 4 -> 0, of which waited for: 3 -> 0; matrix products, arithmetic and copies ran while one was open for 49% -> 0% of each run, Pallas kernels for 0% -> 0%
where the time goes in v1:
time: 99.5 us; the launch traced here: 99 us
  Pallas kernels  91.7 us (92%)
  local copies, waits for them, and re-layouts  7.29 us (7%)
    pallas_call x1, Pallas kernels, body(): pl.pallas_call(functools.partial(kernel, nz, row_peers, line_peers), out_...  91.7 us
    unnamed x25, local copies, waits for them, and re-layouts  7.29 us

profile of v1, /device:TPU:1, one launch (start us, length us, event | category | flops | bytes accessed | tf_op | source)
XLA Modules:
  0.0 99.0 jit_solution(15980220753472097257)
XLA Ops:
  0.0 0.0 copy-start.9
  0.0 0.7 copy-done.9
  0.7 0.0 copy-start.10
  0.7 0.1 copy.12.cn
  0.8 0.6 copy-done.10
  1.4 0.0 copy-start.5
  1.4 0.0 copy-start.6
  1.4 0.0 copy-start.7
  1.4 0.0 copy-start.8
  1.4 0.1 copy.13.cwi
  1.5 0.6 copy-done.5
  2.1 0.0 copy-done.6
  2.1 0.0 copy-done.7
  2.1 0.0 copy-done.8
  2.1 0.0 copy-start
  2.1 1.1 %copy-done = bf16[16,16,1280]{2,1,0:T(8,128)(2,1)S(1)} copy-done((bf16[16,16,1280]{2,1,0:T(8,128)(2,1)S(1)}, bf16[16,16,1280]{2,1,0:T(8,128)(2,1)}, u32[]{:S(2)}) %copy-start) | copy-done | bytes 655384
  3.2 0.0 copy-start.1
  3.2 1.0 %copy-done.1 = bf16[6,64,512]{2,1,0:T(8,128)(2,1)S(1)} copy-done((bf16[6,64,512]{2,1,0:T(8,128)(2,1)S(1)}, bf16[6,64,512]{2,1,0:T(8,128)(2,1)}, u32[]{:S(2)}) %copy-start.1) | copy-done | bytes 393240
  4.2 0.0 copy-start.2
  4.2 1.0 copy-done.2
  5.1 0.0 copy-start.3
  5.1 0.8 copy-done.3
  5.9 0.0 copy-start.4
  5.9 0.8 copy-done.4
  6.7 91.7 %interpolate.1 = bf16[16,4096]{1,0:T(8,128)(2,1)S(1)} custom-call(bf16[256,1280]{1,0:T(8,128)(2,1)S(1)} %bitcast.5, bf16[128,1280]{1,0:T(8,128)(2,1)S(1)} %bitcast.7, bf16[6,64,512]{2,1,0:T(8,128)(2,1)S(1)} %copy-done.1, f32[64,8]{1,0:T(8,128)S(1)} %bitcast.8, f32[64,8]{1,0:T(8,128)S(1)} %bitcast.9, s32[1,8]{1,0:T(1,128)S(1)} %copy-done.6, ...), custom_call_target="tpu_custom_call" | custom-call | tf_op jit(solution)/shard_map/interpolate/pallas_call | solution.py:367
  98.3 0.7 copy.15
Async XLA Ops:
  0.0 0.7 copy-start.9
  0.7 0.7 copy-start.10
  1.4 0.7 copy-start.5
  1.4 0.7 copy-start.6
  1.4 0.7 copy-start.7
  1.4 0.7 copy-start.8
  2.1 1.1 %copy-start = (bf16[16,16,1280]{2,1,0:T(8,128)(2,1)S(1)}, bf16[16,16,1280]{2,1,0:T(8,128)(2,1)}, u32[]{:S(2)}) copy-start(bf16[16,16,1280]{2,1,0:T(8,128)(2,1)} %param.11) | copy-start | bytes 1966084
  3.2 1.0 %copy-start.1 = (bf16[6,64,512]{2,1,0:T(8,128)(2,1)S(1)}, bf16[6,64,512]{2,1,0:T(8,128)(2,1)}, u32[]{:S(2)}) copy-start(bf16[6,64,512]{2,1,0:T(8,128)(2,1)} %tiles_hbm.1) | copy-start | bytes 1179652
  4.2 1.0 copy-start.2
  5.1 0.8 copy-start.3
  5.9 0.8 copy-start.4

commit v2 on v1

v2 whole, which is shorter than its diff:
```python
import functools
import math

import jax
import jax.numpy as jnp
from jax import lax
from jax.experimental import pallas as pl
from jax.experimental.pallas import tpu as pltpu
from jax.sharding import PartitionSpec as P

MESH = pl.DeviceIdType.MESH
PLANE_WAVES = 40960
CORNERS = 8
PAIRS = 64
BANDS = 16
F32 = jnp.float32
BF16 = jnp.bfloat16
NC = 2
NEAR = 5
SLOTS = 4


def lanes(shape):
    return lax.broadcasted_iota(jnp.int32, shape, len(shape) - 1)


def kernel(
    nz, nx, ny,
    fine_hbm, coarse_hbm, tiles_hbm, rv, rc, rn, rwi, cn, cwi, tl, wt,
    out,
    fine, waves, far_w, dense, stack, left, near_t, spread, expanded, rsm, mixed, picked_w, picked_t, sel, from_core,
    part, from_x, sum1, from_y, full, off_d, off_l, wgt, rank, first,
    in_sem, ws, wr, up_s, up_r, ts, tr, far_s, far_r, core_s, core_r, x_s, x_r, y_s, y_r,
):
    g, z = lax.axis_index("ga"), lax.axis_index("ka")
    ng = 2 * nx * ny
    half = nz // 2
    last = half - 2
    assert NEAR == last - 1
    piece = waves.shape[1] // NC
    core = lax.rem(g, 2)
    y, x = g // (2 * nx), lax.rem(g // 2, nx)
    partner = g + 1 - 2 * core

    def away(way, n):
        return lax.rem(z + (n if way == 0 else nz - n), nz)

    nbr = (away(0, 1), away(1, 1))

    get_coarse = pltpu.make_async_copy(coarse_hbm, waves.at[0], in_sem.at[0])
    get_tiles = pltpu.make_async_copy(tiles_hbm, stack.at[pl.ds(0, 6)], in_sem.at[1])
    get_fine = pltpu.make_async_copy(fine_hbm, fine, in_sem.at[2])
    get_coarse.start()
    get_tiles.start()
    get_fine.start()

    def x_peer(r):
        return y * (2 * nx) + 2 * lax.rem(x + r, nx) + core

    def y_peer(r):
        return lax.rem(y + r, ny) * (2 * nx) + 2 * x + core

    up_to, up_from = lax.rem(g + ng - 1, ng), lax.rem(g + 1, ng)
    barrier = pltpu.get_barrier_semaphore()
    friends = [(g, away(way, n)) for n in range(1, half - NEAR + 1) for way in range(2)]
    friends += [(up_to, z), (up_from, z), (partner, z)]
    friends += [(x_peer(r), z) for r in range(1, nx)]
    friends += [(y_peer(r), z) for r in range(1, ny)]
    for who in friends:
        pl.semaphore_signal(barrier, inc=1, device_id=who, device_id_type=MESH)
    pl.semaphore_wait(barrier, len(friends))

    def slot(way, d):
        return lax.rem(nz - d, nz) if way == 0 else d

    def wave(way, d, j):
        cols = pl.ds(j * piece, piece)
        whole = waves.at[slot(way, d), cols]
        return pltpu.make_async_remote_copy(
            src_ref=waves.at[slot(way, d - 1), cols],
            dst_ref=far_w.at[way, cols] if isinstance(d, int) and d == last else whole,
            send_sem=ws.at[way, d - 1, j],
            recv_sem=wr.at[way, d - 1, j],
            device_id=(g, nbr[way]),
            device_id_type=MESH,
        )

    def chosen_wave(way, onward):
        cols = pl.ds(SLOTS, SLOTS // 2) if onward else pl.ds(0, SLOTS)
        j = 0 if onward else 1
        return pltpu.make_async_remote_copy(
            src_ref=picked_w.at[way, cols],
            dst_ref=waves.at[slot(way, half - 1), cols],
            send_sem=ws.at[way, half - 2, j],
            recv_sem=wr.at[way, half - 2, j],
            device_id=(g, nbr[way]),
            device_id_type=MESH,
        )

    def last_wave(way):
        return pltpu.make_async_remote_copy(
            src_ref=waves.at[slot(way, half - 1), pl.ds(SLOTS, SLOTS // 2)],
            dst_ref=waves.at[half, pl.ds(way * (SLOTS // 2), SLOTS // 2)],
            send_sem=ws.at[way, half - 1, 0],
            recv_sem=wr.at[way, half - 1, 0],
            device_id=(g, nbr[way]),
            device_id_type=MESH,
        )

    def tile(way, k):
        whole = left.at[pl.ds(slot(way, k) * 4, 4)]
        return pltpu.make_async_remote_copy(
            src_ref=left.at[pl.ds(slot(way, k - 1) * 4, 4)],
            dst_ref=near_t.at[way, pl.ds(0, 4)] if isinstance(k, int) and k == NEAR else whole,
            send_sem=ts.at[way, k - 1],
            recv_sem=tr.at[way, k - 1],
            device_id=(g, nbr[way]),
            device_id_type=MESH,
        )

    def far_tile(way, k):
        begin, count = (0, 2) if k < half else (way, 1)
        return pltpu.make_async_remote_copy(
            src_ref=picked_t.at[way, k - NEAR - 1, pl.ds(begin, count)],
            dst_ref=left.at[pl.ds(slot(way, k) * 4 + begin, count)],
            send_sem=far_s.at[way, k - NEAR - 1],
            recv_sem=far_r.at[way, k - NEAR - 1],
            device_id=(g, away(way, k - NEAR)),
            device_id_type=MESH,
        )

    def swap(base, count):
        for q in range(count):
            v = left[base + q].astype(F32)
            left[nz * 4 + base + q] = pltpu.roll(v, 64, 1).astype(BF16)

    def correlate(s, j, way=None):
        block = waves[s, pl.ds(j * 4, 4)] if way is None else far_w[way, pl.ds(j * 4, 4)]
        rows = block.reshape(4 * BANDS, waves.shape[3])
        both = lax.dot_general(
            rows, fine[...], (((1,), (1,)), ((), ())), preferred_element_type=F32
        )
        dense[pl.ds(s * 16 + j * 8, 8)] = both.reshape(8, 8, 256)

    get_coarse.wait()
    for jj in range(NC):
        for way in range(2):
            wave(way, 1, jj).start()
    get_tiles.wait()
    upper = pltpu.make_async_remote_copy(
        src_ref=stack.at[pl.ds(0, 6)],
        dst_ref=stack.at[pl.ds(6, 6)],
        send_sem=up_s,
        recv_sem=up_r,
        device_id=(up_to, z),
        device_id_type=MESH,
    )
    upper.start()
    get_fine.wait()
    for j in range(2):
        correlate(0, j)

    scale = 1.0 / (PLANE_WAVES * math.sqrt(PAIRS))

    def ranks(n, carry):
        before, count = carry
        holder = lax.shift_right_logical(tl[z, n], 3)
        count = jnp.where(holder == before, count + 1, 0)
        rank[n] = count
        return holder, count

    lax.fori_loop(0, tl.shape[1], ranks, (jnp.int32(-1), jnp.int32(0)))

    def place(i, carry):
        f, c = i // CORNERS, i % CORNERS
        n = cn[c, f]
        col = tl[z, n]
        s = (lax.shift_right_logical(col, 3) - z + nz) & (nz - 1)
        hops = jnp.minimum(s, nz - s)
        jj = jnp.where(hops > last, rank[n], col & 7)
        off_d[i] = (s * 8 + jj) * 2
        jj = jnp.where(hops > NEAR, rank[n], col & 7)
        off_l[i] = s * 4 + lax.shift_right_logical(jj, 1) + ((jj + c) & 1) * (nz * 4)
        wgt[i] = wt[cwi[c, f]] * scale
        return carry

    lax.fori_loop(0, 128, place, 0)

    into = lanes((128, 1024))
    row = lax.broadcasted_iota(jnp.int32, (128, 1024), 0)
    local = into % 512
    wanted = (local // 64) * 16 + jnp.where(into < 512, (local % 64) // 8, 8 + local % 8)
    spread[...] = jnp.where(row == wanted, 1.0, 0.0).astype(BF16)

    def wave_step(d):
        for jj in range(NC):
            for way in range(2):
                wave(way, d, jj).wait_recv()
                wave(way, d + 1, jj).start()
            if (jj + 1) * piece % 4 == 0:
                for way in range(2):
                    correlate(slot(way, d), (jj + 1) * piece // 4 - 1)

    wave_step(1)

    wide = lanes((8, PAIRS))
    low = lax.broadcasted_iota(jnp.int32, (8, PAIRS), 0)
    to_w = jnp.where(wide // 8 == low, 1.0, 0.0)
    to_y = jnp.where(wide % 8 == low, 1.0, 0.0)
    exact = lax.Precision.HIGHEST
    row_v = jnp.dot(rv[...], to_w, precision=exact, preferred_element_type=F32)
    row_c = jnp.dot(rc[...], to_y, precision=exact, preferred_element_type=F32)
    upper.wait_recv()
    rotated = jnp.zeros((PAIRS, stack.shape[2]), F32)
    for c in range(CORNERS):
        w = wt[rwi[0, c]]
        cond = row_c[c * 8 : c * 8 + 8]
        mat = jnp.concatenate(
            [row_v[c * 8 + v : c * 8 + v + 1] * cond for v in range(8)], axis=0
        )
        mat = (w * mat * (1.0 / math.sqrt(PAIRS))).astype(BF16)
        rotated += jnp.dot(mat, stack[rn[0, c]], preferred_element_type=F32)
    rotated = rotated.astype(BF16)
    for q in range(4):
        left[q] = rotated[:, q * 128 : (q + 1) * 128]
    swap(0, 4)

    def tile_step(k):
        for way in range(2):
            tile(way, k - 1).wait_recv()
        for way in range(2):
            tile(way, k).start()
        for way in range(2):
            swap(slot(way, k - 1) * 4, 4)

    served = []
    for way in range(2):
        served += [(away(way, n), away(1 - way, last)) for n in (1, 2)]
        served += [(away(way, n), away(1 - way, NEAR)) for n in range(1, half - NEAR + 1)]
    per_way = len(served) // 2

    def starts(n, counts):
        return tuple(
            count + jnp.where(lax.shift_right_logical(tl[o, n], 3) < h, 1, 0)
            for count, (o, h) in zip(counts, served)
        )

    counts = lax.fori_loop(0, tl.shape[1], starts, (jnp.int32(0),) * len(served))
    for i, count in enumerate(counts):
        first[i] = count

    def entry(i, k):
        return tl[served[i][0], jnp.minimum(first[i] + k, tl.shape[1] - 1)] & 7

    for way in range(2):
        tile(way, 1).start()

    def both(d, carry):
        wave_step(d)
        tile_step(d)
        return carry

    lax.fori_loop(2, NEAR, both, 0)
    wave_step(NEAR)
    tile_step(NEAR)
    for way in range(2):
        for jj in range(NC):
            wave(way, last, jj).wait_recv()
    near = lanes((64, 128)) < 64
    for way in range(2):
        for n, (owner, k) in enumerate(
            [(0, k) for k in range(SLOTS)] + [(1, way * 2), (1, way * 2 + 1)]
        ):
            picked_w[way, n] = far_w[way, entry(way * per_way + owner, k)]
    for way in range(2):
        chosen_wave(way, True).start()
    for way in range(2):
        chosen_wave(way, False).start()
    for way in range(2):
        for j in range(2):
            correlate(slot(way, last), j, way)

    for way in range(2):
        tile(way, NEAR).wait_recv()
    for way in range(2):
        s = slot(way, NEAR)
        for q in range(4):
            v = near_t[way, q]
            turned = pltpu.roll(v.astype(F32), 64, 1).astype(BF16)
            near_t[way, 4 + q] = turned
            left[s * 4 + q] = v
            left[nz * 4 + s * 4 + q] = turned
        for n in range(half - NEAR):
            for q in range(2):
                lo = entry(way * per_way + 2 + n, 2 * q)
                hi = entry(way * per_way + 2 + n, 2 * q + 1)
                a = near_t[way, lax.shift_right_logical(lo, 1) + (lo & 1) * 4]
                b = near_t[way, lax.shift_right_logical(hi, 1) + ((hi + 1) & 1) * 4]
                picked_t[way, n, q] = jnp.where(near, a, b)
    for way in range(2):
        chosen_wave(way, True).wait_recv()
        last_wave(way).start()
    for way in range(2):
        chosen_wave(way, False).wait_recv()
        correlate(slot(way, half - 1), 0)
    for way in range(2):
        last_wave(way).wait_recv()
    correlate(half, 0)

    for k in range(half, NEAR, -1):
        for way in range(2):
            far_tile(way, k).start()

    lane = lanes((8, 128))

    def pick(c, carry):
        for t in range(2):
            acc = jnp.zeros((8, 128), F32)
            for ff in range(8):
                i = (t * 8 + ff) * CORNERS + c
                val = dense[off_d[i], :, t * 128 : t * 128 + 128] * wgt[i]
                cond = dense[off_d[i] + 1, :, t * 128 : t * 128 + 128]
                acc = jnp.where(lane // 8 == 2 * ff, val, acc)
                acc = jnp.where(lane // 8 == 2 * ff + 1, cond, acc)
            sel[c, :, pl.ds(t * 128, 128)] = acc
        return carry

    lax.fori_loop(0, CORNERS, pick, 0)

    to_core = pltpu.make_async_remote_copy(
        src_ref=sel.at[pl.ds((1 - core) * nx, nx)],
        dst_ref=from_core,
        send_sem=core_s.at[0],
        recv_sem=core_r.at[0],
        device_id=(partner, z),
        device_id_type=MESH,
    )

    def to_x(r):
        return pltpu.make_async_remote_copy(
            src_ref=part,
            dst_ref=from_x.at[r - 1],
            send_sem=x_s.at[r - 1],
            recv_sem=x_r.at[r - 1],
            device_id=(x_peer(r), z),
            device_id_type=MESH,
        )

    def to_y(r):
        return pltpu.make_async_remote_copy(
            src_ref=sum1,
            dst_ref=from_y.at[r - 1],
            send_sem=y_s.at[r - 1],
            recv_sem=y_r.at[r - 1],
            device_id=(y_peer(r), z),
            device_id_type=MESH,
        )

    def across(arriving=False):
        mine = 1 - core if arriving else core
        return pltpu.make_async_remote_copy(
            src_ref=full.at[pl.ds(core * nx, nx)],
            dst_ref=full.at[pl.ds(mine * nx, nx)],
            send_sem=core_s.at[1],
            recv_sem=core_r.at[1],
            device_id=(partner, z),
            device_id_type=MESH,
        )

    to_core.start()
    to_core.wait_recv()
    total = sel[pl.ds(core * nx, nx)] + from_core[...]
    part[...] = total
    for r in range(1, nx):
        to_x(r).start()
    for r in range(1, nx):
        to_x(r).wait_recv()
        total += from_x[r - 1]
    sum1[...] = total
    for r in range(1, ny):
        to_y(r).start()
    for r in range(1, ny):
        to_y(r).wait_recv()
        total += from_y[r - 1]
    full[pl.ds(core * nx, nx)] = total
    across().start()
    for k in range(NEAR + 1, half):
        for way in range(2):
            far_tile(way, k).wait_recv()
            swap(slot(way, k) * 4, 2)
    for way in range(2):
        far_tile(way, half).wait_recv()
    swap(half * 4, 2)
    across(True).wait_recv()

    corr = full[...].reshape(CORNERS * 8, 256)
    corr = jnp.concatenate([corr[:, :128], corr[:, 128:]], axis=0)
    high = corr.astype(BF16)
    rest = (corr - high.astype(F32)).astype(BF16)
    expanded[...] = jnp.dot(high, spread[...], preferred_element_type=F32) + jnp.dot(
        rest, spread[...], preferred_element_type=F32
    )

    def rotate(c, carry):
        for t in range(2):
            at = pl.multiple_of(t * 64 + c * 8, 8)
            val = expanded[pl.ds(at, 8), pl.ds(0, 512)]
            cond = expanded[pl.ds(at, 8), pl.ds(512, 512)]
            for w in range(0, 8, 2):
                both_w = jnp.concatenate([val[w : w + 1] * cond, val[w + 1 : w + 2] * cond], 0)
                to = pl.multiple_of(c * 64 + w * 8, 16)
                rsm[pl.ds(to, 16), pl.ds(t * 512, 512)] = both_w.astype(BF16)
        return carry

    lax.fori_loop(0, CORNERS, rotate, 0)

    for p in range(8):
        blocks = []
        for ff in range(2):
            f = p * 2 + ff
            quads = []
            for q in range(4):
                a = left[off_l[f * CORNERS + 2 * q]]
                b = left[off_l[f * CORNERS + 2 * q + 1]]
                quads.append(jnp.where(near, a, b))
            blocks.append(jnp.concatenate(quads, axis=1))
        res = jnp.dot(
            jnp.concatenate(blocks, axis=0),
            rsm[:, p * 128 : (p + 1) * 128],
            preferred_element_type=F32,
        )
        turned = pltpu.roll(res, 64, 1)
        mixed[p * 128 : p * 128 + 64, :] = jnp.where(near, res[:64], turned[:64])
        mixed[p * 128 + 64 : p * 128 + 128, :] = jnp.where(near, turned[64:], res[64:])

    near_f = lanes((16, 128)) < 64
    for t in range(32):
        even = mixed[pl.ds(2 * t, 16, stride=64), :]
        odd = mixed[pl.ds(2 * t + 1, 16, stride=64), :]
        out[:, t * 128 : (t + 1) * 128] = jnp.where(near_f, even, odd).astype(BF16)

    upper.wait_send()

    def sent(d, carry):
        for way in range(2):
            for j in range(NC):
                wave(way, d, j).wait_send()

            @pl.when(d <= NEAR)
            def _():
                tile(way, d).wait_send()

        return carry

    lax.fori_loop(1, last + 1, sent, 0)
    for way in range(2):
        chosen_wave(way, True).wait_send()
        chosen_wave(way, False).wait_send()
        last_wave(way).wait_send()
        for k in range(NEAR + 1, half + 1):
            far_tile(way, k).wait_send()
    to_core.wait_send()
    for r in range(1, nx):
        to_x(r).wait_send()
    for r in range(1, ny):
        to_y(r).wait_send()
    across().wait_send()


def body(mesh_shape, *args):
    (fine_waves, coarse_waves, coarse_kernel, row_valence, row_conduction, row_neighbours,
     row_weight_index, col_neighbours, col_weight_index, tile_list, weight_table) = args
    nz, ng = mesh_shape
    nx = CORNERS // 2
    ny = ng // CORNERS
    width = fine_waves.shape[2]
    held = coarse_waves.shape[0]
    any_space = pl.BlockSpec(memory_space=pl.ANY)
    vmem = pl.BlockSpec(memory_space=pltpu.VMEM)
    smem = pl.BlockSpec(memory_space=pltpu.SMEM)
    half = nz // 2
    dma = pltpu.SemaphoreType.DMA
    out = pl.pallas_call(
        functools.partial(kernel, nz, nx, ny),
        out_shape=jax.ShapeDtypeStruct((16, PAIRS * PAIRS), BF16),
        in_specs=[any_space] * 3 + [vmem] * 2 + [smem] * 6,
        out_specs=vmem,
        scratch_shapes=[
            pltpu.VMEM((256, width), BF16),
            pltpu.VMEM((nz, held, BANDS, width), BF16),
            pltpu.VMEM((2, held, BANDS, width), BF16),
            pltpu.VMEM((nz * held * 2, 8, 256), F32),
            pltpu.VMEM((12, PAIRS, 512), BF16),
            pltpu.VMEM((2 * nz * 4, PAIRS, 128), BF16),
            pltpu.VMEM((2, 8, PAIRS, 128), BF16),
            pltpu.VMEM((128, 1024), BF16),
            pltpu.VMEM((128, 1024), F32),
            pltpu.VMEM((512, 1024), BF16),
            pltpu.VMEM((1024, 128), F32),
            pltpu.VMEM((2, SLOTS * 3 // 2, BANDS, width), BF16),
            pltpu.VMEM((2, half - NEAR, 2, PAIRS, 128), BF16),
            pltpu.VMEM((CORNERS, 8, 256), F32),
            pltpu.VMEM((nx, 8, 256), F32),
            pltpu.VMEM((nx, 8, 256), F32),
            pltpu.VMEM((nx - 1, nx, 8, 256), F32),
            pltpu.VMEM((nx, 8, 256), F32),
            pltpu.VMEM((ny - 1, nx, 8, 256), F32),
            pltpu.VMEM((CORNERS, 8, 256), F32),
            pltpu.SMEM((128,), jnp.int32),
            pltpu.SMEM((128,), jnp.int32),
            pltpu.SMEM((128,), F32),
            pltpu.SMEM((32,), jnp.int32),
            pltpu.SMEM((32,), jnp.int32),
            dma((3,)),
            dma((2, half, NC)),
            dma((2, half, NC)),
            dma,
            dma,
            dma((2, NEAR)),
            dma((2, NEAR)),
            dma((2, half - NEAR)),
            dma((2, half - NEAR)),
            dma((2,)),
            dma((2,)),
            dma((nx - 1,)),
            dma((nx - 1,)),
            dma((ny - 1,)),
            dma((ny - 1,)),
        ],
        compiler_params=pltpu.CompilerParams(
            collective_id=0, has_side_effects=True, vmem_limit_bytes=60 * 1024 * 1024
        ),
        name="interpolate",
    )(
        fine_waves.reshape(16 * BANDS, width),
        coarse_waves,
        coarse_kernel,
        row_valence.reshape(64, 8),
        row_conduction.reshape(64, 8),
        row_neighbours,
        row_weight_index,
        col_neighbours.T,
        col_weight_index.T,
        tile_list,
        weight_table,
    )
    return out[None]


def solution(mesh):
    placed = (
        P("ka", None, "ga"),
        P("ka", None, "ga"),
        P("ga", None, "ka"),
        P("ga", None, None, None),
        P("ga", None, None, None),
        P("ga", None),
        P("ga", None),
        P("ka", None),
        P("ka", None),
        P(),
        P(),
    )
    shape = (mesh.shape["ka"], mesh.shape["ga"])
    return jax.shard_map(
        functools.partial(body, shape),
        mesh=mesh,
        in_specs=placed,
        out_specs=P("ga", "ka", None),
        check_vma=False,
    )
```

time: 99.5 us -> 90.3 us (0.908)
  local copies, waits for them, and re-layouts: 7.29 us -> 1.57 us
  Pallas kernels: 91.7 us -> 88.5 us
    unnamed x25 -> x1, local copies, waits for them, and re-layouts: 7.29 us -> 1.57 us
    pallas_call x1, Pallas kernels: 91.7 us -> 88.5 us  [body(): pl.pallas_call(functools.partial(kernel, nz, nx, ny), out_shape=jax.Shape...]
where the time goes in v2:
time: 90.3 us; the launch traced here: 90.1 us
  Pallas kernels  88.5 us (98%)
  local copies, waits for them, and re-layouts  1.57 us (2%)
    pallas_call x1, Pallas kernels, body(): pl.pallas_call(functools.partial(kernel, nz, nx, ny), out_shape=jax.Shape...  88.5 us

profile of v2, /device:TPU:1, one launch (start us, length us, event | category | flops | bytes accessed | tf_op | source)
XLA Modules:
  0.0 90.1 jit_solution(18256816115747413913)
XLA Ops:
  0.0 88.5 %interpolate.1 = bf16[16,4096]{1,0:T(8,128)(2,1)} custom-call(bf16[256,1280]{1,0:T(8,128)(2,1)} %bitcast.6, bf16[8,16,1280]{2,1,0:T(8,128)(2,1)} %coarse_hbm.1, bf16[6,64,512]{2,1,0:T(8,128)(2,1)} %tiles_hbm.1, f32[64,8]{1,0:T(8,128)} %bitcast.8, f32[64,8]{1,0:T(8,128)} %bitcast.9, s32[1,8]{1,0:T(1,128)} %rn.1, s32[1,8]{1,0:T(1,128)} %rwi.1, ...), custom_call_target="tpu_custom_call" | custom-call | tf_op jit(solution)/shard_map/interpolate/pallas_call | solution.py:483
  88.5 1.6 %copy.13 = bf16[1,16,4096]{2,1,0:T(8,128)(2,1)} copy(bf16[1,16,4096]{2,1,0:T(8,128)(2,1)} %bitcast.7) | data formatting | bytes 262144

commit v3 on v2

--- a/solution.py
+++ b/solution.py
@@ -26,8 +26,9 @@
 
 def kernel(
     nz, nx, ny,
-    fine_hbm, coarse_hbm, tiles_hbm, rv, rc, rn, rwi, cn, cwi, tl, wt,
+    fine_hbm, coarse_hbm, tiles_hbm, rv_hbm, rc_hbm, rn_hbm, rwi_hbm, cn_hbm, cwi_hbm, tl_hbm, wt_hbm,
     out,
+    rv, rc, rn, rwi, cn, cwi, tl, wt,
     fine, waves, far_w, dense, stack, left, near_t, spread, expanded, rsm, mixed, picked_w, picked_t, sel, from_core,
     part, from_x, sum1, from_y, full, off_d, off_l, wgt, rank, first,
     in_sem, ws, wr, up_s, up_r, ts, tr, far_s, far_r, core_s, core_r, x_s, x_r, y_s, y_r,
@@ -53,6 +54,13 @@
     get_coarse.start()
     get_tiles.start()
     get_fine.start()
+    small = ((rv_hbm, rv), (rc_hbm, rc), (rn_hbm, rn), (rwi_hbm, rwi), (cn_hbm, cn), (cwi_hbm, cwi))
+    small += ((tl_hbm, tl), (wt_hbm, wt))
+    get_small = [
+        pltpu.make_async_copy(src, dst, in_sem.at[3 + i]) for i, (src, dst) in enumerate(small)
+    ]
+    for copy in get_small:
+        copy.start()
 
     def x_peer(r):
         return y * (2 * nx) + 2 * lax.rem(x + r, nx) + core
@@ -157,6 +165,8 @@
     )
     upper.start()
     get_fine.wait()
+    for copy in get_small:
+        copy.wait()
     for j in range(2):
         correlate(0, j)
 
@@ -391,28 +401,34 @@
     for way in range(2):
         far_tile(way, half).wait_recv()
     swap(half * 4, 2)
+    def rotations(side):
+        rows = nx * 8
+        corr = full[pl.ds(side * nx, nx)].reshape(rows, 256)
+        corr = jnp.concatenate([corr[:, :128], corr[:, 128:]], axis=0)
+        high = corr.astype(BF16)
+        rest = (corr - high.astype(F32)).astype(BF16)
+        expanded[...] = jnp.dot(high, spread[...], preferred_element_type=F32) + jnp.dot(
+            rest, spread[...], preferred_element_type=F32
+        )
+
+        def rotate(c, carry):
+            for t in range(2):
+                at = pl.multiple_of(t * rows + c * 8, 8)
+                val = expanded[pl.ds(at, 8), pl.ds(0, 512)]
+                cond = expanded[pl.ds(at, 8), pl.ds(512, 512)]
+                for w in range(0, 8, 2):
+                    both_w = jnp.concatenate(
+                        [val[w : w + 1] * cond, val[w + 1 : w + 2] * cond], 0
+                    )
+                    to = pl.multiple_of((side * nx + c) * 64 + w * 8, 16)
+                    rsm[pl.ds(to, 16), pl.ds(t * 512, 512)] = both_w.astype(BF16)
+            return carry
+
+        lax.fori_loop(0, nx, rotate, 0)
+
+    rotations(core)
     across(True).wait_recv()
-
-    corr = full[...].reshape(CORNERS * 8, 256)
-    corr = jnp.concatenate([corr[:, :128], corr[:, 128:]], axis=0)
-    high = corr.astype(BF16)
-    rest = (corr - high.astype(F32)).astype(BF16)
-    expanded[...] = jnp.dot(high, spread[...], preferred_element_type=F32) + jnp.dot(
-        rest, spread[...], preferred_element_type=F32
-    )
-
-    def rotate(c, carry):
-        for t in range(2):
-            at = pl.multiple_of(t * 64 + c * 8, 8)
-            val = expanded[pl.ds(at, 8), pl.ds(0, 512)]
-            cond = expanded[pl.ds(at, 8), pl.ds(512, 512)]
-            for w in range(0, 8, 2):
-                both_w = jnp.concatenate([val[w : w + 1] * cond, val[w + 1 : w + 2] * cond], 0)
-                to = pl.multiple_of(c * 64 + w * 8, 16)
-                rsm[pl.ds(to, 16), pl.ds(t * 512, 512)] = both_w.astype(BF16)
-        return carry
-
-    lax.fori_loop(0, CORNERS, rotate, 0)
+    rotations(1 - core)
 
     for p in range(8):
         blocks = []
@@ -477,15 +493,23 @@
     held = coarse_waves.shape[0]
     any_space = pl.BlockSpec(memory_space=pl.ANY)
     vmem = pl.BlockSpec(memory_space=pltpu.VMEM)
-    smem = pl.BlockSpec(memory_space=pltpu.SMEM)
+    smem = pltpu.SMEM
     half = nz // 2
     dma = pltpu.SemaphoreType.DMA
     out = pl.pallas_call(
         functools.partial(kernel, nz, nx, ny),
         out_shape=jax.ShapeDtypeStruct((16, PAIRS * PAIRS), BF16),
-        in_specs=[any_space] * 3 + [vmem] * 2 + [smem] * 6,
+        in_specs=[any_space] * 11,
         out_specs=vmem,
         scratch_shapes=[
+            pltpu.VMEM((64, 8), F32),
+            pltpu.VMEM((64, 8), F32),
+            smem((1, CORNERS), jnp.int32),
+            smem((1, CORNERS), jnp.int32),
+            smem((CORNERS, 16), jnp.int32),
+            smem((CORNERS, 16), jnp.int32),
+            smem(tile_list.shape, jnp.int32),
+            smem(weight_table.shape, F32),
             pltpu.VMEM((256, width), BF16),
             pltpu.VMEM((nz, held, BANDS, width), BF16),
             pltpu.VMEM((2, held, BANDS, width), BF16),
@@ -494,7 +518,7 @@
             pltpu.VMEM((2 * nz * 4, PAIRS, 128), BF16),
             pltpu.VMEM((2, 8, PAIRS, 128), BF16),
             pltpu.VMEM((128, 1024), BF16),
-            pltpu.VMEM((128, 1024), F32),
+            pltpu.VMEM((64, 1024), F32),
             pltpu.VMEM((512, 1024), BF16),
             pltpu.VMEM((1024, 128), F32),
             pltpu.VMEM((2, SLOTS * 3 // 2, BANDS, width), BF16),
@@ -511,7 +535,7 @@
             pltpu.SMEM((128,), F32),
             pltpu.SMEM((32,), jnp.int32),
             pltpu.SMEM((32,), jnp.int32),
-            dma((3,)),
+            dma((11,)),
             dma((2, half, NC)),
             dma((2, half, NC)),
             dma,

time: 90.3 us -> 89 us (0.986)
  Pallas kernels: 88.5 us -> 87.3 us
    pallas_call x1, Pallas kernels: 88.5 us -> 87.3 us  [body(): pl.pallas_call(functools.partial(kernel, nz, nx, ny), out_shape=jax.Shape...]
where the time goes in v3:
time: 89 us; the launch traced here: 88.8 us
  Pallas kernels  87.3 us (98%)
  local copies, waits for them, and re-layouts  1.57 us (2%)
    pallas_call x1, Pallas kernels, body(): pl.pallas_call(functools.partial(kernel, nz, nx, ny), out_shape=jax.Shape...  87.3 us

profile of v3, /device:TPU:1, one launch (start us, length us, event | category | flops | bytes accessed | tf_op | source)
XLA Modules:
  0.0 88.8 jit_solution(2527885110659869048)
XLA Ops:
  0.0 87.3 %interpolate.1 = bf16[16,4096]{1,0:T(8,128)(2,1)} custom-call(bf16[256,1280]{1,0:T(8,128)(2,1)} %bitcast.6, bf16[8,16,1280]{2,1,0:T(8,128)(2,1)} %coarse_hbm.1, bf16[6,64,512]{2,1,0:T(8,128)(2,1)} %tiles_hbm.1, f32[64,8]{1,0:T(8,128)} %bitcast.8, f32[64,8]{1,0:T(8,128)} %bitcast.9, s32[1,8]{1,0:T(1,128)} %rn_hbm.1, s32[1,8]{1,0:T(1,128)} %rwi_hbm.1, ...), custom_call_target="tpu_custom_call" | custom-call | tf_op jit(solution)/shard_map/interpolate/pallas_call | solution.py:499
  87.3 1.6 %copy.13 = bf16[1,16,4096]{2,1,0:T(8,128)(2,1)} copy(bf16[1,16,4096]{2,1,0:T(8,128)(2,1)} %bitcast.7) | data formatting | bytes 262144

commit v4 on v3

--- a/solution.py
+++ b/solution.py
@@ -31,7 +31,7 @@
     rv, rc, rn, rwi, cn, cwi, tl, wt,
     fine, waves, far_w, dense, stack, left, near_t, spread, expanded, rsm, mixed, picked_w, picked_t, sel, from_core,
     part, from_x, sum1, from_y, full, off_d, off_l, wgt, rank, first,
-    in_sem, ws, wr, up_s, up_r, ts, tr, far_s, far_r, core_s, core_r, x_s, x_r, y_s, y_r,
+    in_sem, ws, wr, up_s, up_r, ts, tr, far_s, far_r, core_s, core_r, x_s, x_r, y_s, y_r, word,
 ):
     g, z = lax.axis_index("ga"), lax.axis_index("ka")
     ng = 2 * nx * ny
@@ -70,13 +70,21 @@
 
     up_to, up_from = lax.rem(g + ng - 1, ng), lax.rem(g + 1, ng)
     barrier = pltpu.get_barrier_semaphore()
-    friends = [(g, away(way, n)) for n in range(1, half - NEAR + 1) for way in range(2)]
-    friends += [(up_to, z), (up_from, z), (partner, z)]
-    friends += [(x_peer(r), z) for r in range(1, nx)]
-    friends += [(y_peer(r), z) for r in range(1, ny)]
+    friends = [(g, nbr[0]), (g, nbr[1]), (up_to, z), (up_from, z)]
     for who in friends:
         pl.semaphore_signal(barrier, inc=1, device_id=who, device_id_type=MESH)
     pl.semaphore_wait(barrier, len(friends))
+
+    steps = ((1, 0), (2, 0), (4, 0), (8, 0), (0, 1), (0, 1))
+
+    def pass_word(i):
+        by_g, by_z = steps[i]
+        for sign in (1, -1):
+            who = (lax.rem(g + sign * by_g + ng, ng), lax.rem(z + sign * by_z + nz, nz))
+            pl.semaphore_signal(word.at[i], inc=1, device_id=who, device_id_type=MESH)
+
+    def hear_word(i):
+        pl.semaphore_wait(word.at[i], 2)
 
     def slot(way, d):
         return lax.rem(nz - d, nz) if way == 0 else d
@@ -154,6 +162,8 @@
     for jj in range(NC):
         for way in range(2):
             wave(way, 1, jj).start()
+    pass_word(0)
+    pass_word(4)
     get_tiles.wait()
     upper = pltpu.make_async_remote_copy(
         src_ref=stack.at[pl.ds(0, 6)],
@@ -211,6 +221,10 @@
                 for way in range(2):
                     correlate(slot(way, d), (jj + 1) * piece // 4 - 1)
 
+    hear_word(0)
+    hear_word(4)
+    pass_word(1)
+    pass_word(5)
     wave_step(1)
 
     wide = lanes((8, PAIRS))
@@ -270,9 +284,15 @@
         tile_step(d)
         return carry
 
+    hear_word(1)
+    hear_word(5)
+    pass_word(2)
     lax.fori_loop(2, NEAR, both, 0)
+    hear_word(2)
+    pass_word(3)
     wave_step(NEAR)
     tile_step(NEAR)
+    hear_word(3)
     for way in range(2):
         for jj in range(NC):
             wave(way, last, jj).wait_recv()
@@ -323,19 +343,20 @@
 
     lane = lanes((8, 128))
 
-    def pick(c, carry):
+    def pick(i, side):
+        c = side * nx + i
         for t in range(2):
             acc = jnp.zeros((8, 128), F32)
             for ff in range(8):
-                i = (t * 8 + ff) * CORNERS + c
-                val = dense[off_d[i], :, t * 128 : t * 128 + 128] * wgt[i]
-                cond = dense[off_d[i] + 1, :, t * 128 : t * 128 + 128]
+                n = (t * 8 + ff) * CORNERS + c
+                val = dense[off_d[n], :, t * 128 : t * 128 + 128] * wgt[n]
+                cond = dense[off_d[n] + 1, :, t * 128 : t * 128 + 128]
                 acc = jnp.where(lane // 8 == 2 * ff, val, acc)
                 acc = jnp.where(lane // 8 == 2 * ff + 1, cond, acc)
             sel[c, :, pl.ds(t * 128, 128)] = acc
-        return carry
-
-    lax.fori_loop(0, CORNERS, pick, 0)
+        return side
+
+    lax.fori_loop(0, nx, pick, 1 - core)
 
     to_core = pltpu.make_async_remote_copy(
         src_ref=sel.at[pl.ds((1 - core) * nx, nx)],
@@ -378,6 +399,7 @@
         )
 
     to_core.start()
+    lax.fori_loop(0, nx, pick, core)
     to_core.wait_recv()
     total = sel[pl.ds(core * nx, nx)] + from_core[...]
     part[...] = total
@@ -426,28 +448,34 @@
 
         lax.fori_loop(0, nx, rotate, 0)
 
+    def products(side, add):
+        for p in range(8):
+            blocks = []
+            for ff in range(2):
+                at = (p * 2 + ff) * CORNERS + side * nx
+                quads = []
+                for q in range(2):
+                    a, b = left[off_l[at + 2 * q]], left[off_l[at + 2 * q + 1]]
+                    quads.append(jnp.where(near, a, b))
+                blocks.append(jnp.concatenate(quads, axis=1))
+            res = jnp.dot(
+                jnp.concatenate(blocks, axis=0),
+                rsm[pl.ds(side * 256, 256), p * 128 : (p + 1) * 128],
+                preferred_element_type=F32,
+            )
+            if add:
+                res += mixed[p * 128 : (p + 1) * 128]
+                turned = pltpu.roll(res, 64, 1)
+                even = jnp.where(near, res[:64], turned[:64])
+                odd = jnp.where(near, turned[64:], res[64:])
+                res = jnp.concatenate([even, odd], axis=0)
+            mixed[p * 128 : (p + 1) * 128] = res
+
     rotations(core)
+    products(core, False)
     across(True).wait_recv()
     rotations(1 - core)
-
-    for p in range(8):
-        blocks = []
-        for ff in range(2):
-            f = p * 2 + ff
-            quads = []
-            for q in range(4):
-                a = left[off_l[f * CORNERS + 2 * q]]
-                b = left[off_l[f * CORNERS + 2 * q + 1]]
-                quads.append(jnp.where(near, a, b))
-            blocks.append(jnp.concatenate(quads, axis=1))
-        res = jnp.dot(
-            jnp.concatenate(blocks, axis=0),
-            rsm[:, p * 128 : (p + 1) * 128],
-            preferred_element_type=F32,
-        )
-        turned = pltpu.roll(res, 64, 1)
-        mixed[p * 128 : p * 128 + 64, :] = jnp.where(near, res[:64], turned[:64])
-        mixed[p * 128 + 64 : p * 128 + 128, :] = jnp.where(near, turned[64:], res[64:])
+    products(1 - core, True)
 
     near_f = lanes((16, 128)) < 64
     for t in range(32):
@@ -550,6 +578,7 @@
             dma((nx - 1,)),
             dma((ny - 1,)),
             dma((ny - 1,)),
+            pltpu.SemaphoreType.REGULAR((6,)),
         ],
         compiler_params=pltpu.CompilerParams(
             collective_id=0, has_side_effects=True, vmem_limit_bytes=60 * 1024 * 1024

time: 89 us -> 87.6 us (0.984)
  Pallas kernels: 87.3 us -> 85.9 us
    pallas_call x1, Pallas kernels: 87.3 us -> 85.9 us  [body(): pl.pallas_call(functools.partial(kernel, nz, nx, ny), out_shape=jax.Shape...]
where the time goes in v4:
time: 87.6 us; the launch traced here: 87.5 us
  Pallas kernels  85.9 us (98%)
  local copies, waits for them, and re-layouts  1.57 us (2%)
    pallas_call x1, Pallas kernels, body(): pl.pallas_call(functools.partial(kernel, nz, nx, ny), out_shape=jax.Shape...  85.9 us

profile of v4, /device:TPU:1, one launch (start us, length us, event | category | flops | bytes accessed | tf_op | source)
XLA Modules:
  0.0 87.5 jit_solution(8121958843779283233)
XLA Ops:
  0.0 85.9 %interpolate.1 = bf16[16,4096]{1,0:T(8,128)(2,1)} custom-call(bf16[256,1280]{1,0:T(8,128)(2,1)} %bitcast.6, bf16[8,16,1280]{2,1,0:T(8,128)(2,1)} %coarse_hbm.1, bf16[6,64,512]{2,1,0:T(8,128)(2,1)} %tiles_hbm.1, f32[64,8]{1,0:T(8,128)} %bitcast.8, f32[64,8]{1,0:T(8,128)} %bitcast.9, s32[1,8]{1,0:T(1,128)} %rn_hbm.1, s32[1,8]{1,0:T(1,128)} %rwi_hbm.1, ...), custom_call_target="tpu_custom_call" | custom-call | tf_op jit(solution)/shard_map/interpolate/pallas_call | solution.py:527
  85.9 1.6 %copy.13 = bf16[1,16,4096]{2,1,0:T(8,128)(2,1)} copy(bf16[1,16,4096]{2,1,0:T(8,128)(2,1)} %bitcast.7) | data formatting | bytes 262144

commit v5 on v4

--- a/solution.py
+++ b/solution.py
@@ -27,8 +27,8 @@
 def kernel(
     nz, nx, ny,
     fine_hbm, coarse_hbm, tiles_hbm, rv_hbm, rc_hbm, rn_hbm, rwi_hbm, cn_hbm, cwi_hbm, tl_hbm, wt_hbm,
-    out,
-    rv, rc, rn, rwi, cn, cwi, tl, wt,
+    out_hbm,
+    out, rv, rc, rn, rwi, cn, cwi, tl, wt,
     fine, waves, far_w, dense, stack, left, near_t, spread, expanded, rsm, mixed, picked_w, picked_t, sel, from_core,
     part, from_x, sum1, from_y, full, off_d, off_l, wgt, rank, first,
     in_sem, ws, wr, up_s, up_r, ts, tr, far_s, far_r, core_s, core_r, x_s, x_r, y_s, y_r, word,
@@ -411,6 +411,27 @@
     sum1[...] = total
     for r in range(1, ny):
         to_y(r).start()
+    upper.wait_send()
+
+    def sent(d, carry):
+        for way in range(2):
+            for j in range(NC):
+                wave(way, d, j).wait_send()
+
+            @pl.when(d <= NEAR)
+            def _():
+                tile(way, d).wait_send()
+
+        return carry
+
+    lax.fori_loop(1, last + 1, sent, 0)
+    for way in range(2):
+        chosen_wave(way, True).wait_send()
+        chosen_wave(way, False).wait_send()
+        last_wave(way).wait_send()
+        for k in range(NEAR + 1, half + 1):
+            far_tile(way, k).wait_send()
+
     for r in range(1, ny):
         to_y(r).wait_recv()
         total += from_y[r - 1]
@@ -478,37 +499,24 @@
     products(1 - core, True)
 
     near_f = lanes((16, 128)) < 64
+    def put(i):
+        part_of = pl.ds(i * 1024, 1024)
+        return pltpu.make_async_copy(out.at[:, part_of], out_hbm.at[:, part_of], in_sem.at[i])
+
     for t in range(32):
         even = mixed[pl.ds(2 * t, 16, stride=64), :]
         odd = mixed[pl.ds(2 * t + 1, 16, stride=64), :]
         out[:, t * 128 : (t + 1) * 128] = jnp.where(near_f, even, odd).astype(BF16)
-
-    upper.wait_send()
-
-    def sent(d, carry):
-        for way in range(2):
-            for j in range(NC):
-                wave(way, d, j).wait_send()
-
-            @pl.when(d <= NEAR)
-            def _():
-                tile(way, d).wait_send()
-
-        return carry
-
-    lax.fori_loop(1, last + 1, sent, 0)
-    for way in range(2):
-        chosen_wave(way, True).wait_send()
-        chosen_wave(way, False).wait_send()
-        last_wave(way).wait_send()
-        for k in range(NEAR + 1, half + 1):
-            far_tile(way, k).wait_send()
+        if t % 8 == 7:
+            put(t // 8).start()
     to_core.wait_send()
     for r in range(1, nx):
         to_x(r).wait_send()
     for r in range(1, ny):
         to_y(r).wait_send()
     across().wait_send()
+    for i in range(4):
+        put(i).wait()
 
 
 def body(mesh_shape, *args):
@@ -520,7 +528,6 @@
     width = fine_waves.shape[2]
     held = coarse_waves.shape[0]
     any_space = pl.BlockSpec(memory_space=pl.ANY)
-    vmem = pl.BlockSpec(memory_space=pltpu.VMEM)
     smem = pltpu.SMEM
     half = nz // 2
     dma = pltpu.SemaphoreType.DMA
@@ -528,8 +535,9 @@
         functools.partial(kernel, nz, nx, ny),
         out_shape=jax.ShapeDtypeStruct((16, PAIRS * PAIRS), BF16),
         in_specs=[any_space] * 11,
-        out_specs=vmem,
+        out_specs=any_space,
         scratch_shapes=[
+            pltpu.VMEM((16, PAIRS * PAIRS), BF16),
             pltpu.VMEM((64, 8), F32),
             pltpu.VMEM((64, 8), F32),
             smem((1, CORNERS), jnp.int32),

time: 87.6 us -> 87.5 us (level)
  no operation moved by 1% of the time
where the time goes in v5:
time: 87.5 us; the launch traced here: 87.4 us
  Pallas kernels  85.8 us (98%)
  local copies, waits for them, and re-layouts  1.57 us (2%)
    pallas_call x1, Pallas kernels, body(): pl.pallas_call(functools.partial(kernel, nz, nx, ny), out_shape=jax.Shape...  85.8 us

profile of v5, /device:TPU:1, one launch (start us, length us, event | category | flops | bytes accessed | tf_op | source)
XLA Modules:
  0.0 87.4 jit_solution(8933267779339467072)
XLA Ops:
  0.0 85.8 %interpolate.1 = bf16[16,4096]{1,0:T(8,128)(2,1)} custom-call(bf16[256,1280]{1,0:T(8,128)(2,1)} %bitcast.6, bf16[8,16,1280]{2,1,0:T(8,128)(2,1)} %coarse_hbm.1, bf16[6,64,512]{2,1,0:T(8,128)(2,1)} %tiles_hbm.1, f32[64,8]{1,0:T(8,128)} %bitcast.8, f32[64,8]{1,0:T(8,128)} %bitcast.9, s32[1,8]{1,0:T(1,128)} %rn_hbm.1, s32[1,8]{1,0:T(1,128)} %rwi_hbm.1, ...), custom_call_target="tpu_custom_call" | custom-call | tf_op jit(solution)/shard_map/interpolate/pallas_call | solution.py:534
  85.8 1.6 %copy.13 = bf16[1,16,4096]{2,1,0:T(8,128)(2,1)} copy(bf16[1,16,4096]{2,1,0:T(8,128)(2,1)} %bitcast.7) | data formatting | bytes 262144
